TPU v7x, 32 devices: a whole 2x2x4 slice. The times are simulated.
32 devices in a mesh: seq: 8 (over z, y), head: 4 (over x, core).
Axes of the slice: x: 2, y: 2, z: 4, core: 2. Of those that a mesh axis runs over, the one named last changes fastest.
Arguments:
- inputs: bfloat16 [2048, 5120], P('seq', 'head'), may hold values from -6 to 6
- time_step: float32 [80, 2048], P('head', 'seq'), may hold values from 0.01 to 0.3
- decay_rate: float32 [80], P('head'), may hold values from 0.0001 to 1
- input_map: bfloat16 [2048, 128], P('seq'), may hold values from -6 to 6
- output_map: bfloat16 [2048, 128], P('seq'), may hold values from -0.59765625 to 0.59765625
- output_grad: bfloat16 [2048, 5120], P('seq', 'head'), may hold values from -3 to 3
- span_states: float32 [8, 80, 64, 128], P('seq', 'head'), may hold values from -6 to 6
- resets: int32 [8], P('seq'), may hold values from 0 to 4095
Outputs:
- grad_inputs: bfloat16 [2048, 5120], P('seq', 'head')
- grad_input_map: float32 [2048, 128], P('seq')
- grad_rate: float32 [80], P('head')
Inputs may be any that keep to these rules, and one draw needn't show every extreme that they name: `resets`: A value p under 256 means that a document starts at position p of that span; a value of 256 or more means that none starts in it.
All inputs are finite; a program needn't handle non-finite values.
Results may differ from a plain program's by a relative error of at most 0.003.
Values sent between devices are 32-bit elements; how exact they have to be, the bound alone decides.
A program may use at most 64 MiB of HBM per device.

v0:
```python
import jax
import jax.numpy as jnp
from jax import lax
from jax.sharding import PartitionSpec as P

highest = lax.Precision.HIGHEST


def prepare(x_block, step_block, decay_rate, b_block, c_block, grad_block, start_state, reset_at):
    block_len = step_block.shape[1]
    positions = jnp.arange(block_len, dtype=jnp.int32)
    later_doc = positions >= reset_at
    no_reset = reset_at >= block_len
    elapsed = jnp.cumsum(step_block, axis=1)
    log_decay = -decay_rate[:, None] * elapsed
    joined = (later_doc[:, None] == later_doc[None, :]) & (positions[None, :] >= positions[:, None])
    log_gaps = log_decay[:, None, :] - log_decay[:, :, None]
    pair_weight = jnp.where(joined[None], jnp.exp(jnp.where(joined[None], log_gaps, 0.0)), 0.0)
    intersection = jnp.dot(b_block, c_block.T, preferred_element_type=jnp.float32)
    products = jnp.einsum("shp,uhp->hsu", x_block, grad_block, preferred_element_type=jnp.float32)
    mixing = (pair_weight * intersection[None]).astype(jnp.bfloat16)
    pair_terms = pair_weight * products
    paired = pair_terms.astype(jnp.bfloat16)
    dx_inner = jnp.einsum("hsu,uhp->shp", mixing, grad_block, preferred_element_type=jnp.float32)
    db_inner = jnp.einsum("hsu,un->hsn", paired, c_block, preferred_element_type=jnp.float32)
    start_weight = jnp.where(later_doc[None], 0.0, jnp.exp(log_decay))
    end_weight = jnp.where(
        (later_doc | no_reset)[None], jnp.exp(log_decay[:, -1:] - log_decay), 0.0
    )
    carry_gain = jnp.where(no_reset, jnp.exp(log_decay[:, -1]), 0.0)
    c_wide = c_block.astype(jnp.float32)
    grad_wide = grad_block.astype(jnp.float32)
    weighted_c = start_weight[:, :, None] * c_wide[None]
    boundary_grad = jnp.einsum("hun,uhp->hpn", weighted_c, grad_wide, precision=highest)
    state_read = jnp.einsum("uhp,hpn->hun", grad_wide, start_state, precision=highest)
    start_term = jnp.sum(state_read * c_wide[None], axis=2)
    inside_term = jnp.sum(
        pair_terms
        * intersection[None]
        * step_block[:, :, None]
        * (elapsed[:, None, :] - elapsed[:, :, None]),
        axis=(1, 2),
    )
    entry_term = jnp.sum(start_weight * elapsed * start_term, axis=1)
    return (
        carry_gain,
        boundary_grad,
        dx_inner,
        db_inner,
        inside_term + entry_term,
        end_weight,
        elapsed,
    )


def finish(prepared, x_block, step_block, b_block, start_state, carried):
    carry_gain, boundary_grad, dx_inner, db_inner, partial_rate, end_weight, elapsed = prepared
    b_wide = b_block.astype(jnp.float32)
    x_wide = x_block.astype(jnp.float32)
    carried_b = jnp.einsum("sn,hpn->shp", b_wide, carried, precision=highest)
    carried_x = jnp.einsum("shp,hpn->hsn", x_wide, carried, precision=highest)
    step_rows = step_block.T[:, :, None]
    end_rows = end_weight.T[:, :, None]
    grad_x = (step_rows * (dx_inner + end_rows * carried_b)).astype(jnp.bfloat16)
    grad_b = jnp.sum(
        step_block[:, :, None] * (db_inner + end_weight[:, :, None] * carried_x), axis=0
    )
    last_elapsed = elapsed[:, -1]
    leaving_term = jnp.sum(
        end_weight
        * step_block
        * (last_elapsed[:, None] - elapsed)
        * jnp.sum(carried_x * b_wide[None], axis=2),
        axis=1,
    )
    through_term = carry_gain * last_elapsed * jnp.sum(carried * start_state, axis=(1, 2))
    return (grad_x, grad_b, partial_rate + leaving_term + through_term)


def backward_step(running, members):
    grad_piece, gain_piece = members
    return (grad_piece + gain_piece[:, None] * running, running)


def body(inputs, time_step, decay_rate, input_map, output_map, output_grad, span_states, resets):
    length = time_step.shape[1]
    block_count = span_states.shape[0]
    block_len = length // block_count
    head_count = decay_rate.shape[0]
    head_width = inputs.shape[1] // head_count
    number = 0
    x_block = inputs.reshape(block_len, head_count, head_width)
    grad_block = output_grad.reshape(block_len, head_count, head_width)
    step_block = time_step
    b_block = input_map
    prepared = prepare(
        x_block,
        step_block,
        decay_rate,
        b_block,
        output_map,
        grad_block,
        span_states[number],
        resets[number],
    )
    pieces = [(prepared, x_block, step_block, b_block)]
    gain_total = jnp.ones((head_count,), jnp.float32)
    grad_total = jnp.zeros_like(span_states[0])
    for number in reversed(range(block_count)):
        gain_block, grad_block_sum = (pieces[number][0][0], pieces[number][0][1])
        grad_total = grad_block_sum + gain_block[:, None, None] * grad_total
        gain_total = gain_block * gain_total
    seq_count = lax.axis_size("seq")
    entries = grad_total.shape[1] * grad_total.shape[2]
    sliced = grad_total.reshape(head_count, seq_count, entries // seq_count)
    received = lax.all_to_all(sliced, "seq", split_axis=1, concat_axis=1, tiled=True)
    gains = lax.all_gather(gain_total[None], "seq", axis=0, tiled=True)
    ending, exclusive = lax.scan(
        backward_step,
        jnp.zeros_like(received[:, 0]),
        (jnp.transpose(received, (1, 0, 2)), gains),
        reverse=True,
    )
    returned = lax.all_to_all(
        jnp.transpose(exclusive, (1, 0, 2)), "seq", split_axis=1, concat_axis=1, tiled=True
    )
    incoming = returned.reshape(grad_total.shape)
    carried = incoming
    grad_x_list = [None] * block_count
    grad_b_list = [None] * block_count
    rate_total = jnp.zeros((head_count,), jnp.float32)
    for number in reversed(range(block_count)):
        prepared, x_block, step_block, b_block = pieces[number]
        grad_x, grad_b, rate_part = finish(
            prepared, x_block, step_block, b_block, span_states[number], carried
        )
        grad_x_list[number] = grad_x.reshape(block_len, head_count * head_width)
        grad_b_list[number] = grad_b
        rate_total = rate_part
        carried = prepared[1] + prepared[0][:, None, None] * carried
    grad_inputs = grad_x_list[0]
    grad_input_map = lax.psum(grad_b_list[0], "head")
    grad_rate = -lax.psum(rate_total, "seq")
    return (grad_inputs, grad_input_map, grad_rate)


def solution(mesh):
    in_specs = (
        P("seq", "head"),
        P("head", "seq"),
        P("head"),
        P("seq", None),
        P("seq", None),
        P("seq", "head"),
        P("seq", "head", None, None),
        P("seq"),
    )
    out_specs = (P("seq", "head"), P("seq", None), P("head"))
    return jax.shard_map(body, mesh=mesh, in_specs=in_specs, out_specs=out_specs, check_vma=False)
```

profile of v0, /device:TPU:0, one launch (start us, length us, event | category | flops | bytes accessed | tf_op | source)
XLA Modules:
  0.0 141.0 jit_solution(17333116644024165966)
XLA Ops:
  8.6 0.8 reshape.290
  11.2 0.9 copy.37
  12.2 1.4 copy.36
  13.6 1.7 %fusion.31 = f32[20,64,128]{2,1,0:T(8,128)S(1)} fusion(bf16[256,20,64]{0,2,1:T(8,128)(2,1)S(1)} %bitcast.80, f32[256,128]{0,1:T(8,128)S(1)} %copy.37, f32[20,256]{1,0:T(8,128)S(1)} %get-tuple-element.152, f32[20]{0:T(128)S(1)} %broadcast_multiply_fusion.1), kind=kOutput, calls=%fused_computation.38 | convolution fusion | flops 504135680 | bytes 1462352 | tf_op jit(solution)/shard_map/hun,uhp->hpn/dot_general | solution.py:34
  15.4 1.3 copy.39
  16.7 7.3 %all-to-all-start = ((f32[20,8,1024]{2,0,1:T(8,128)}), f32[20,8,1024]{2,0,1:T(8,128)S(1)}, u32[]{:S(2)}, u32[]{:S(2)}) async-start(f32[20,8,1024]{2,0,1:T(8,128)} %copy.39), calls=%async_computation | async-start | bytes 1572864 | tf_op jit(solution)/shard_map/all_to_all | solution.py:116
  25.6 26.1 %all-reduce = f32[160]{0:T(256)S(1)} all-reduce(f32[160]{0:T(256)S(1)} %dynamic-update-slice), channel_id=2, replica_groups=mesh['seq'=8,'head'=4] {'seq'}, use_global_device_ids=true, to_apply=%add | all-reduce | flops 160 | bytes 1280
  53.9 0.7 slice_reduce_fusion.1
  54.7 1.4 %fusion.37 = pred[256,256]{1,0:T(8,128)(4,1)} fusion(pred[256]{0:T(512)(128)(4,1)} %copy-done.10), kind=kLoop, calls=%fused_computation.42 | loop fusion | flops 196608 | bytes 65792 | tf_op jit(solution)/shard_map/and | solution.py:16
  56.1 1.8 %fusion.43 = f32[256,256]{1,0:T(8,128)} fusion(bf16[256,128]{1,0:T(8,128)(2,1)} %param.13, bf16[256,128]{1,0:T(8,128)(2,1)} %param.14), kind=kOutput, calls=%fused_computation.64 | convolution fusion | flops 16777216 | bytes 393216 | tf_op jit(solution)/shard_map/dot_general | solution.py:19
  57.9 1.0 broadcast_in_dim.97
  58.9 11.4 %while.17 = (s32[]{:T(128)}, f32[20,1024]{1,0:T(8,128)S(1)}, f32[8,20,1024]{2,1,0:T(8,128)}, f32[8,20,1024]{2,1,0:T(8,128)S(1)}, f32[8,20]{1,0:T(8,128)}, /*index=5*/s32[]{:T(128)}, s32[]{:T(128)}, s32[]{:T(128)}) while((s32[]{:T(128)}, f32[20,1024]{1,0:T(8,128)S(1)}, f32[8,20,1024]{2,1,0:T(8,128)}, f32[8,20,1024]{2,1,0:T(8,128)S(1)}, ...), condition=%wide.region_3.4_spmd.clone, body=%wide.region_2.3_spmd.clone.sunk | while | flops 81924 | bytes 426352 | solution.py:118
  60.3 0.7 fusion.55
  61.7 0.7 fusion.55
  63.1 0.7 fusion.55
  64.6 0.7 fusion.55
  66.0 0.7 fusion.55
  67.4 0.7 fusion.55
  68.9 0.7 fusion.55
  70.3 4.5 %all-to-all-start.1 = ((f32[20,8,1024]{2,0,1:T(8,128)}), f32[20,8,1024]{2,0,1:T(8,128)S(1)}, u32[]{:S(2)}, u32[]{:S(2)}) async-start(f32[20,8,1024]{2,0,1:T(8,128)} %bitcast.8), calls=%async_computation.1 | async-start | bytes 1572864 | tf_op jit(solution)/shard_map/all_to_all | solution.py:124
  74.8 2.8 %multiply_reduce_fusion.1 = f32[20,256]{1,0:T(8,128)} fusion(bf16[256,20,64]{0,2,1:T(8,128)(2,1)S(1)} %bitcast.81, f32[256,128]{0,1:T(8,128)} %copy-done.7, f32[1,20,64,128]{3,2,1,0:T(8,128)S(1)} %copy-done.2), kind=kOutput, calls=%fused_computation.17 | convolution fusion | flops 504622080 | bytes 1462272 | tf_op jit(solution)/shard_map/uhp,hpn->hun/dot_general | solution.py:35
  77.7 3.7 %fusion.21 = f32[256,20,64]{0,2,1:T(8,128)} fusion(bf16[256,20,64]{0,2,1:T(8,128)(2,1)S(1)} %bitcast.82, f32[256,256]{1,0:T(8,128)} %fusion.43, f32[20,256]{1,0:T(8,128)S(1)} %get-tuple-element.153, pred[256,256]{1,0:T(8,128)(4,1)} %fusion.37), kind=kOutput, calls=%fused_computation.29 | convolution fusion | flops 174325760 | bytes 2314240 | tf_op jit(solution)/shard_map/hsu,uhp->shp/dot_general | solution.py:24
  81.4 5.3 %multiply_reduce_fusion = (f32[20]{0:T(128)}, f32[20,256,256]{2,1,0:T(8,128)}) fusion(f32[20,256]{1,0:T(8,128)S(1)} %bitcast.86, f32[20,256]{1,0:T(8,128)S(1)} %copy-done.6, f32[256,256]{1,0:T(8,128)S(1)} %copy-done.5, f32[20,256]{1,0:T(8,128)S(1)} %get-tuple-element.153, pred[256,256]{1,0:T(8,128)(4,1)S(1)} %copy-done.8, ...), kind=kOutput, calls=%fused_computation.4 | convolution fusion | flops 179568624 | bytes 6942800 | tf_op jit(solution)/shard_map/shp,uhp->hsu/dot_general | solution.py:20
  86.8 5.5 %all-to-all-done.1 = f32[20,8,1024]{2,0,1:T(8,128)S(1)} async-done(((f32[20,8,1024]{2,0,1:T(8,128)}), f32[20,8,1024]{2,0,1:T(8,128)S(1)}, u32[]{:S(2)}, u32[]{:S(2)}) %all-to-all-start.1) | async-done | bytes 655392 | tf_op jit(solution)/shard_map/all_to_all | solution.py:124
  92.3 1.1 multiply_reduce_fusion.2
  93.4 2.8 %fusion.9 = (f32[20,256]{1,0:T(8,128)S(1)}, f32[20,128,256]{1,2,0:T(8,128)S(1)}) fusion(f32[256,128]{1,0:T(8,128)} %convert_element_type.21, f32[20,64,128]{2,1,0:T(8,128)S(1)} %reshape.294, bf16[256,20,64]{0,2,1:T(8,128)(2,1)S(1)} %bitcast.77), kind=kOutput, calls=%fused_computation.16 | convolution fusion | flops 504622080 | bytes 4083712 | tf_op jit(solution)/shard_map/shp,hpn->hsn/dot_general | solution.py:61
  96.5 5.2 %fusion.8 = f32[256,128]{1,0:T(8,128)} fusion(f32[20,128,256]{1,2,0:T(8,128)S(1)} %get-tuple-element.155, f32[20,256]{1,0:T(8,128)S(1)} %get-tuple-element.150, f32[20,256]{1,0:T(8,128)S(1)} %copy-done.6, f32[20,256,256]{2,1,0:T(8,128)} %get-tuple-element.157, f32[20,256]{1,0:T(8,128)S(1)} %get-tuple-element.153, pred[256,256]{1,0:T(8,128)(4,1)} %fusion.37, ...), kind=kOutput, calls=%fused_computation.15 | convolution fusion | flops 344686592 | bytes 8187904 | tf_op jit(solution)/shard_map/hsu,un->hsn/dot_general | solution.py:25
  101.8 0.7 fusion.25
  102.4 19.4 %psum.15 = f32[20]{0:T(128)S(1)} all-reduce(f32[20]{0:T(128)S(1)} %multiply_add_fusion), channel_id=1, replica_groups=mesh['seq'=8,'head'=4] {'seq'}, use_global_device_ids=true, to_apply=%region_12.13 | all-reduce | flops 20 | bytes 160 | tf_op jit(solution)/shard_map/psum | solution.py:143
  121.8 1.1 copy.44
  123.4 9.1 %all-reduce.3.cloned.1.call-done = f32[256,128]{1,0:T(8,128)} async-done(((f32[256,128]{1,0:T(8,128)}), f32[256,128]{1,0:T(8,128)}) %all-reduce.3.cloned.1.call-update) | async-done | bytes 131088 | tf_op jit(solution)/shard_map/psum | solution.py:142
  132.6 1.6 %copy.62 = f32[256,128]{1,0:T(8,128)} copy(f32[256,128]{1,0:T(8,128)} %all-reduce.3.cloned.1.call-done) | data formatting | bytes 262144
  (90 shorter events, 13.1 us)
Async XLA Ops:
  7.2 16.8 %copy-start.20 = (u32[32]{0:T(128)S(1)}, u32[32]{0:T(128)}, u32[]{:S(2)}) copy-start(u32[32]{0:T(128)} %constant.57) | copy-start | bytes 388
  7.2 45.2 %copy-start.3 = (bf16[256,128]{1,0:T(8,128)(2,1)S(1)}, bf16[256,128]{1,0:T(8,128)(2,1)}, u32[]{:S(2)}) copy-start(bf16[256,128]{1,0:T(8,128)(2,1)} %param.13) | copy-start | bytes 196612
  7.2 45.8 %copy-start.1 = (bf16[256,1280]{1,0:T(8,128)(2,1)S(1)}, bf16[256,1280]{1,0:T(8,128)(2,1)}, u32[]{:S(2)}) copy-start(bf16[256,1280]{1,0:T(8,128)(2,1)} %param.10) | copy-start | bytes 1966084
  7.2 46.0 %copy-start.2 = (f32[1,20,64,128]{3,2,1,0:T(8,128)S(1)}, f32[1,20,64,128]{3,2,1,0:T(8,128)}, u32[]{:S(2)}) copy-start(f32[1,20,64,128]{3,2,1,0:T(8,128)} %param.16) | copy-start | bytes 1966084
  8.6 43.7 %copy-start.14 = (f32[20]{0:T(128)}, f32[20]{0:T(128)S(1)}, u32[]{:S(2)}) copy-start(f32[20]{0:T(128)S(1)} %neg.7) | copy-start | bytes 244
  10.9 41.4 %copy-start.10 = (pred[256]{0:T(512)(128)(4,1)}, pred[256]{0:T(512)(128)(4,1)S(1)}, u32[]{:S(2)}) copy-start(pred[256]{0:T(512)(128)(4,1)S(1)} %get-tuple-element.158) | copy-start | bytes 772
  11.2 41.1 %copy-start.11 = (f32[20]{0:T(128)}, f32[20]{0:T(128)S(1)}, u32[]{:S(2)}) copy-start(f32[20]{0:T(128)S(1)} %get-tuple-element.137) | copy-start | bytes 244
  12.2 1.4 copy-start.7
  16.7 41.2 %all-to-all-start = ((f32[20,8,1024]{2,0,1:T(8,128)}), f32[20,8,1024]{2,0,1:T(8,128)S(1)}, u32[]{:S(2)}, u32[]{:S(2)}) async-start(f32[20,8,1024]{2,0,1:T(8,128)} %copy.39), calls=%async_computation | async-start | bytes 1572864 | tf_op jit(solution)/shard_map/all_to_all | solution.py:116
  70.3 22.0 %all-to-all-start.1 = ((f32[20,8,1024]{2,0,1:T(8,128)}), f32[20,8,1024]{2,0,1:T(8,128)S(1)}, u32[]{:S(2)}, u32[]{:S(2)}) async-start(f32[20,8,1024]{2,0,1:T(8,128)} %bitcast.8), calls=%async_computation.1 | async-start | bytes 1572864 | tf_op jit(solution)/shard_map/all_to_all | solution.py:124
  74.8 57.8 %all-reduce.3.cloned.1.call-start = ((), (), s32[]{:S(2)}) async-start(), calls=%async_computation.2 | async-start | bytes 262144 | tf_op jit(solution)/shard_map/psum | solution.py:142
  77.7 3.7 %copy-start.5 = (f32[256,256]{1,0:T(8,128)S(1)}, f32[256,256]{1,0:T(8,128)}, u32[]{:S(2)}) copy-start(f32[256,256]{1,0:T(8,128)} %fusion.43) | copy-start | bytes 786436
  77.7 3.7 %copy-start.6 = (f32[20,256]{1,0:T(8,128)S(1)}, f32[20,256]{1,0:T(8,128)}, u32[]{:S(2)}) copy-start(f32[20,256]{1,0:T(8,128)} %param.11) | copy-start | bytes 61444
  77.7 3.7 %copy-start.8 = (pred[256,256]{1,0:T(8,128)(4,1)S(1)}, pred[256,256]{1,0:T(8,128)(4,1)}, u32[]{:S(2)}) copy-start(pred[256,256]{1,0:T(8,128)(4,1)} %fusion.37) | copy-start | bytes 196612
  86.8 9.4 %copy-start.9 = (f32[20,256]{1,0:T(8,128)S(1)}, f32[20,256]{1,0:T(8,128)}, u32[]{:S(2)}) copy-start(f32[20,256]{1,0:T(8,128)} %multiply_reduce_fusion.1) | copy-start | bytes 61444
  86.8 9.4 %copy-start.12 = (f32[20]{0:T(128)S(1)}, f32[20]{0:T(128)}, u32[]{:S(2)}) copy-start(f32[20]{0:T(128)} %copy-done.11) | copy-start | bytes 244
  86.8 9.5 %copy-start.13 = (f32[20]{0:T(128)S(1)}, f32[20]{0:T(128)}, u32[]{:S(2)}) copy-start(f32[20]{0:T(128)} %slice_reduce_fusion.1) | copy-start | bytes 244
  86.8 9.5 %copy-start.15 = (f32[20]{0:T(128)S(1)}, f32[20]{0:T(128)}, u32[]{:S(2)}) copy-start(f32[20]{0:T(128)} %copy-done.14) | copy-start | bytes 244
  86.8 9.5 %copy-start.16 = (pred[256]{0:T(512)(128)(4,1)S(1)}, pred[256]{0:T(512)(128)(4,1)}, u32[]{:S(2)}) copy-start(pred[256]{0:T(512)(128)(4,1)} %get-tuple-element.159) | copy-start | bytes 772
  86.8 9.5 %copy-start.18 = (pred[256]{0:T(512)(128)(4,1)S(1)}, pred[256]{0:T(512)(128)(4,1)}, u32[]{:S(2)}) copy-start(pred[256]{0:T(512)(128)(4,1)} %compare_bitcast_fusion) | copy-start | bytes 772
  96.5 5.2 %copy-start.17 = (f32[20]{0:T(128)S(1)}, f32[20]{0:T(128)}, u32[]{:S(2)}) copy-start(f32[20]{0:T(128)} %get-tuple-element.148) | copy-start | bytes 244
  96.5 5.2 %copy-start.19 = (f32[20]{0:T(128)S(1)}, f32[20]{0:T(128)}, u32[]{:S(2)}) copy-start(f32[20]{0:T(128)} %get-tuple-element.156) | copy-start | bytes 244
  96.5 5.2 %copy-start = (f32[256,20,64]{0,2,1:T(8,128)S(1)}, f32[256,20,64]{0,2,1:T(8,128)}, u32[]{:S(2)}) copy-start(f32[256,20,64]{0,2,1:T(8,128)} %fusion.21) | copy-start | bytes 3932164
  96.5 5.2 %copy-start.4 = (bf16[256,128]{1,0:T(8,128)(2,1)S(1)}, bf16[256,128]{1,0:T(8,128)(2,1)}, u32[]{:S(2)}) copy-start(bf16[256,128]{1,0:T(8,128)(2,1)} %param.13) | copy-start | bytes 196612
Sparse Core Ops, SparseCore 0:
  101.8 30.7 all-reduce.2
where the time goes:
time: 142 us; the launch traced here: 141 us
  blocking collectives  45.5 us (32%)
  matrix products  24 us (17%)
  local copies, waits for them, and re-layouts  16.6 us (12%)
  between operations  15.8 us (11%)
  waiting for transfers between devices  14.6 us (10%)
  other arithmetic  12.4 us (9%)
  starting transfers between devices  11.9 us (8%)
    unnamed x1, blocking collectives  26.1 us
    psum x1, blocking collectives, body(): grad_rate = -lax.psum(rate_total, 'seq')  19.4 us
    psum x1, waiting for transfers between devices, body(): grad_input_map = lax.psum(grad_b_list[0], 'head')  9.15 us
    all_to_all x1, starting transfers between devices, body(): lax.all_to_all(sliced, 'seq', split_axis=1, concat_axis=1, tiled=True)  7.31 us
    mul x8, local copies, waits for them, and re-layouts, backward_step(): return (grad_piece + gain_piece[:, None] * running, running)  5.48 us
    all_to_all x1, waiting for transfers between devices, body(): lax.all_to_all(jnp.transpose(exclusive, (1, 0, 2)), 'seq', split_axis=1,...  5.48 us
    dot_general x1, matrix products, prepare(): jnp.einsum('shp,uhp->hsu', x_block, grad_block, preferred_element_type=jn...  5.34 us
    unnamed x51, local copies, waits for them, and re-layouts  5.26 us
  transfers between devices with their start and end apart: 3, of which 2 were waited for; matrix products, arithmetic and copies ran while one was open for 15% of the time, Pallas kernels for 0%

commit v1 on v0

--- a/solution.py
+++ b/solution.py
@@ -139,7 +139,11 @@
         rate_total = rate_part
         carried = prepared[1] + prepared[0][:, None, None] * carried
     grad_inputs = grad_x_list[0]
-    grad_input_map = lax.psum(grad_b_list[0], "head")
+    grad_input_map = grad_b_list[0]
+    for hop in (1, 2):
+        grad_input_map = grad_input_map + lax.ppermute(
+            grad_input_map, "head", [(dev, dev ^ hop) for dev in range(4)]
+        )
     grad_rate = -lax.psum(rate_total, "seq")
     return (grad_inputs, grad_input_map, grad_rate)
 

time: 142 us -> 122 us (0.86)
  between operations: 15.8 us -> 2.36 us
  waiting for transfers between devices: 14.6 us -> 5.97 us
  other arithmetic: 12.4 us -> 15.2 us
  starting transfers between devices: 11.9 us -> 13.5 us
    psum x1 -> x0, waiting for transfers between devices: 9.15 us -> none  [body(): grad_input_map = lax.psum(grad_b_list[0], 'head')]
    ppermute x0 -> x2, starting transfers between devices: none -> 1.63 us  [body(): lax.ppermute(grad_input_map, 'head', [(dev, dev ^ hop) for dev in range(4)])]
    unnamed x51 -> x52, local copies, waits for them, and re-layouts: 5.26 us -> 4.96 us
  transfers between devices with their start and end apart: 3 -> 4, of which waited for: 2 -> 2; matrix products, arithmetic and copies ran while one was open for 15% -> 20% of each run, Pallas kernels for 0% -> 0%
where the time goes in v1:
time: 122 us; the launch traced here: 121 us
  blocking collectives  44.3 us (36%)
  matrix products  23.3 us (19%)
  local copies, waits for them, and re-layouts  16.2 us (13%)
  other arithmetic  15.2 us (12%)
  starting transfers between devices  13.5 us (11%)
  waiting for transfers between devices  5.97 us (5%)
  between operations  2.36 us (2%)
    unnamed x1, blocking collectives  24.9 us
    psum x1, blocking collectives, body(): grad_rate = -lax.psum(rate_total, 'seq')  19.4 us
    all_to_all x1, starting transfers between devices, body(): lax.all_to_all(sliced, 'seq', split_axis=1, concat_axis=1, tiled=True)  7.31 us
    dot_general x1, matrix products, prepare(): jnp.einsum('shp,uhp->hsu', x_block, grad_block, preferred_element_type=jn...  6.19 us
    mul x8, local copies, waits for them, and re-layouts, backward_step(): return (grad_piece + gain_piece[:, None] * running, running)  5.48 us
    dynamic_update_slice x8, other arithmetic, body(): lax.scan(backward_step, jnp.zeros_like(received[:, 0]), (jnp.transpose(re...  5.13 us
    unnamed x52, local copies, waits for them, and re-layouts  4.96 us
    all_to_all x1, waiting for transfers between devices, body(): lax.all_to_all(jnp.transpose(exclusive, (1, 0, 2)), 'seq', split_axis=1,...  4.66 us
  transfers between devices with their start and end apart: 4, of which 2 were waited for; matrix products, arithmetic and copies ran while one was open for 20% of the time, Pallas kernels for 0%

profile of v1, /device:TPU:0, one launch (start us, length us, event | category | flops | bytes accessed | tf_op | source)
XLA Modules:
  0.0 121.0 jit_solution(13743856752084405102)
XLA Ops:
  2.1 0.8 reshape.290
  4.4 0.8 select_reduce_fusion
  5.2 0.9 copy.37
  6.1 1.4 %copy.36 = bf16[256,1280]{0,1:T(8,128)(2,1)S(1)} copy(bf16[256,1280]{1,0:T(8,128)(2,1)} %param.15) | data formatting | bytes 1310720 | tf_op args[5]
  7.5 1.7 %fusion.31 = f32[20,64,128]{2,1,0:T(8,128)S(1)} fusion(bf16[256,20,64]{0,2,1:T(8,128)(2,1)S(1)} %bitcast.80, f32[256,128]{0,1:T(8,128)S(1)} %copy.37, f32[20,256]{1,0:T(8,128)S(1)} %get-tuple-element.152, f32[20]{0:T(128)S(1)} %broadcast_multiply_fusion.1), kind=kOutput, calls=%fused_computation.38 | convolution fusion | flops 504135680 | bytes 1462352 | tf_op jit(solution)/shard_map/hun,uhp->hpn/dot_general | solution.py:34
  9.4 1.3 %copy.39 = f32[20,8,1024]{2,0,1:T(8,128)} copy(f32[20,8,1024]{2,1,0:T(8,128)S(1)} %reshape.293) | data formatting | bytes 1310720 | tf_op jit(solution)/shard_map/reshape | solution.py:115
  10.6 7.3 %all-to-all-start = ((f32[20,8,1024]{2,0,1:T(8,128)}), f32[20,8,1024]{2,0,1:T(8,128)S(1)}, u32[]{:S(2)}, u32[]{:S(2)}) async-start(f32[20,8,1024]{2,0,1:T(8,128)} %copy.39), calls=%async_computation | async-start | bytes 1572864 | tf_op jit(solution)/shard_map/all_to_all | solution.py:116
  17.9 1.3 %dynamic-slice = u32[1]{0:T(128)} dynamic-slice(u32[32]{0:T(128)} %constant.57, u32[]{:T(128)S(6)} %add.66), dynamic_slice_sizes={1} | dynamic-slice | bytes 12
  19.9 0.9 dynamic-update-slice
  20.7 24.9 %all-reduce = f32[160]{0:T(256)S(1)} all-reduce(f32[160]{0:T(256)S(1)} %dynamic-update-slice), channel_id=2, replica_groups=mesh['seq'=8,'head'=4] {'seq'}, use_global_device_ids=true, to_apply=%add | all-reduce | flops 160 | bytes 1280
  46.3 1.5 %convert_element_type.21 = f32[256,128]{1,0:T(8,128)} convert(bf16[256,128]{1,0:T(8,128)(2,1)} %param.13) | non-fusion elementwise | flops 32768 | bytes 196608 | tf_op jit(solution)/shard_map/convert_element_type | solution.py:58
  48.7 0.7 slice_reduce_fusion.1
  49.4 1.4 %fusion.37 = pred[256,256]{1,0:T(8,128)(4,1)} fusion(pred[256]{0:T(512)(128)(4,1)} %copy-done.13), kind=kLoop, calls=%fused_computation.42 | loop fusion | flops 196608 | bytes 65792 | tf_op jit(solution)/shard_map/and | solution.py:16
  50.8 1.8 %fusion.43 = f32[256,256]{1,0:T(8,128)} fusion(bf16[256,128]{1,0:T(8,128)(2,1)} %param.13, bf16[256,128]{1,0:T(8,128)(2,1)} %param.14), kind=kOutput, calls=%fused_computation.64 | convolution fusion | flops 16777216 | bytes 393216 | tf_op jit(solution)/shard_map/dot_general | solution.py:19
  52.6 1.0 broadcast_in_dim.97
  53.6 11.4 %while.17 = (s32[]{:T(128)}, f32[20,1024]{1,0:T(8,128)S(1)}, f32[8,20,1024]{2,1,0:T(8,128)}, f32[8,20,1024]{2,1,0:T(8,128)S(1)}, f32[8,20]{1,0:T(8,128)}, /*index=5*/s32[]{:T(128)}, s32[]{:T(128)}, s32[]{:T(128)}) while((s32[]{:T(128)}, f32[20,1024]{1,0:T(8,128)S(1)}, f32[8,20,1024]{2,1,0:T(8,128)}, f32[8,20,1024]{2,1,0:T(8,128)S(1)}, ...), condition=%wide.region_3.4_spmd.clone, body=%wide.region_2.3_spmd.clone.sunk | while | flops 81924 | bytes 426352 | solution.py:118
  55.0 0.7 fusion.55
  56.4 0.7 fusion.55
  65.0 4.5 %all-to-all-start.1 = ((f32[20,8,1024]{2,0,1:T(8,128)}), f32[20,8,1024]{2,0,1:T(8,128)S(1)}, u32[]{:S(2)}, u32[]{:S(2)}) async-start(f32[20,8,1024]{2,0,1:T(8,128)} %bitcast.8), calls=%async_computation.1 | async-start | bytes 1572864 | tf_op jit(solution)/shard_map/all_to_all | solution.py:124
  69.5 2.8 %multiply_reduce_fusion.1 = f32[20,256]{1,0:T(8,128)} fusion(bf16[256,20,64]{0,2,1:T(8,128)(2,1)S(1)} %bitcast.81, f32[256,128]{0,1:T(8,128)} %copy-done.10, f32[1,20,64,128]{3,2,1,0:T(8,128)S(1)} %copy-done.2), kind=kOutput, calls=%fused_computation.17 | convolution fusion | flops 504622080 | bytes 1462272 | tf_op jit(solution)/shard_map/uhp,hpn->hun/dot_general | solution.py:35
  72.4 3.7 %fusion.21 = f32[256,20,64]{0,2,1:T(8,128)} fusion(bf16[256,20,64]{0,2,1:T(8,128)(2,1)S(1)} %bitcast.82, f32[256,256]{1,0:T(8,128)} %fusion.43, f32[20,256]{1,0:T(8,128)S(1)} %get-tuple-element.153, pred[256,256]{1,0:T(8,128)(4,1)} %fusion.37), kind=kOutput, calls=%fused_computation.29 | convolution fusion | flops 174325760 | bytes 2314240 | tf_op jit(solution)/shard_map/hsu,uhp->shp/dot_general | solution.py:24
  76.1 6.2 %multiply_reduce_fusion = (f32[20]{0:T(128)}, f32[20,256,256]{2,1,0:T(8,128)}) fusion(f32[20,256]{1,0:T(8,128)S(1)} %bitcast.87, f32[20,256]{1,0:T(8,128)S(1)} %copy-done.8, f32[256,256]{1,0:T(8,128)S(1)} %copy-done.7, f32[20,256]{1,0:T(8,128)} %copy-done.12, pred[256,256]{1,0:T(8,128)(4,1)S(1)} %copy-done.11, bf16[256,20,64]{0,2,1:T(8,128)(2,1)S(1)} %bitcast.76, ...), kind=kOutput, calls=%fused_computation.4 | convolution fusion | flops 179568624 | bytes 6942800 | tf_op jit(solution)/shard_map/shp,uhp->hsu/dot_general | solution.py:20
  82.3 4.7 %all-to-all-done.1 = f32[20,8,1024]{2,0,1:T(8,128)S(1)} async-done(((f32[20,8,1024]{2,0,1:T(8,128)}), f32[20,8,1024]{2,0,1:T(8,128)S(1)}, u32[]{:S(2)}, u32[]{:S(2)}) %all-to-all-start.1) | async-done | bytes 655392 | tf_op jit(solution)/shard_map/all_to_all | solution.py:124
  87.0 1.1 multiply_reduce_fusion.2
  88.2 1.9 %fusion.9 = (f32[20,256]{1,0:T(8,128)S(1)}, f32[20,128,256]{1,2,0:T(8,128)S(1)}) fusion(f32[256,128]{1,0:T(8,128)S(1)} %copy-done.4, f32[20,64,128]{2,1,0:T(8,128)S(1)} %reshape.294, bf16[256,20,64]{0,2,1:T(8,128)(2,1)S(1)} %bitcast.77), kind=kOutput, calls=%fused_computation.16 | convolution fusion | flops 504622080 | bytes 4083712 | tf_op jit(solution)/shard_map/shp,hpn->hsn/dot_general | solution.py:61
  90.1 1.0 multiply_reduce_fusion.4
  91.1 4.5 %fusion.8 = f32[256,128]{1,0:T(8,128)S(1)} fusion(f32[20,128,256]{1,2,0:T(8,128)S(1)} %get-tuple-element.155, f32[20,256]{1,0:T(8,128)S(1)} %get-tuple-element.150, f32[20,256]{1,0:T(8,128)} %param.11, f32[20,256,256]{2,1,0:T(8,128)} %get-tuple-element.157, f32[20,256]{1,0:T(8,128)} %copy-done.12, pred[256,256]{1,0:T(8,128)(4,1)} %fusion.37, ...), kind=kOutput, calls=%fused_computation.15 | convolution fusion | flops 344686592 | bytes 8187904 | tf_op jit(solution)/shard_map/hsu,un->hsn/dot_general | solution.py:25
  95.7 1.3 %collective-permute-done = f32[256,128]{1,0:T(8,128)S(1)} collective-permute-done((f32[256,128]{1,0:T(8,128)S(1)}, f32[256,128]{1,0:T(8,128)S(1)}, u32[]{:S(2)}, u32[]{:S(2)}) %collective-permute-start) | collective-permute-done | bytes 131104 | tf_op jit(solution)/shard_map/ppermute | solution.py:144
  97.1 1.6 %collective-permute-start.1 = (f32[256,128]{1,0:T(8,128)S(1)}, f32[256,128]{1,0:T(8,128)S(1)}, u32[]{:S(2)}, u32[]{:S(2)}) collective-permute-start(f32[256,128]{1,0:T(8,128)S(1)} %add.61), channel_id=1, source_target_pairs={{0,2},{1,3},{2,0},{3,1},{4,6},{5,7},{6,4},{7,5},{8,10},{9,11},{10,... | collective-permute-start | bytes 393224 | tf_op jit(solution)/shard_map/ppermute | solution.py:144
  98.6 0.7 fusion.25
  99.3 19.4 %psum.7 = f32[20]{0:T(128)S(1)} all-reduce(f32[20]{0:T(128)S(1)} %multiply_add_fusion), channel_id=1, replica_groups=mesh['seq'=8,'head'=4] {'seq'}, use_global_device_ids=true, to_apply=%region_11.12 | all-reduce | flops 20 | bytes 160 | tf_op jit(solution)/shard_map/psum | solution.py:147
  118.7 1.1 copy.44
  (94 shorter events, 15.2 us)
Async XLA Ops:
  0.6 47.2 %copy-start.1 = (bf16[256,1280]{1,0:T(8,128)(2,1)S(1)}, bf16[256,1280]{1,0:T(8,128)(2,1)}, u32[]{:S(2)}) copy-start(bf16[256,1280]{1,0:T(8,128)(2,1)} %param.10) | copy-start | bytes 1966084
  0.6 47.4 %copy-start.2 = (f32[1,20,64,128]{3,2,1,0:T(8,128)S(1)}, f32[1,20,64,128]{3,2,1,0:T(8,128)}, u32[]{:S(2)}) copy-start(f32[1,20,64,128]{3,2,1,0:T(8,128)} %param.16) | copy-start | bytes 1966084
  2.1 2.3 %copy-start.17 = (f32[20]{0:T(128)}, f32[20]{0:T(128)S(1)}, u32[]{:S(2)}) copy-start(f32[20]{0:T(128)S(1)} %neg.7) | copy-start | bytes 244
  3.8 44.9 %copy-start.5 = (f32[3,8,2,128]{3,1,2,0:T(8,128)}, f32[3,8,2,128]{3,1,2,0:T(8,128)S(1)}, u32[]{:S(2)}) copy-start(f32[3,8,2,128]{3,1,2,0:T(8,128)S(1)} %copy.47) | copy-start | bytes 73732
  4.3 3.2 %copy-start.13 = (pred[256]{0:T(512)(128)(4,1)}, pred[256]{0:T(512)(128)(4,1)S(1)}, u32[]{:S(2)}) copy-start(pred[256]{0:T(512)(128)(4,1)S(1)} %get-tuple-element.158) | copy-start | bytes 772
  4.4 68.0 %copy-start.12 = (f32[20,256]{1,0:T(8,128)}, f32[20,256]{1,0:T(8,128)S(1)}, u32[]{:S(2)}) copy-start(f32[20,256]{1,0:T(8,128)S(1)} %get-tuple-element.153) | copy-start | bytes 61444
  5.1 2.4 %copy-start.14 = (f32[20]{0:T(128)}, f32[20]{0:T(128)S(1)}, u32[]{:S(2)}) copy-start(f32[20]{0:T(128)S(1)} %get-tuple-element.137) | copy-start | bytes 244
  6.1 4.5 %copy-start.10 = (f32[256,128]{0,1:T(8,128)}, f32[256,128]{0,1:T(8,128)S(1)}, u32[]{:S(2)}) copy-start(f32[256,128]{0,1:T(8,128)S(1)} %copy.37) | copy-start | bytes 393220
  10.6 42.0 %all-to-all-start = ((f32[20,8,1024]{2,0,1:T(8,128)}), f32[20,8,1024]{2,0,1:T(8,128)S(1)}, u32[]{:S(2)}, u32[]{:S(2)}) async-start(f32[20,8,1024]{2,0,1:T(8,128)} %copy.39), calls=%async_computation | async-start | bytes 1572864 | tf_op jit(solution)/shard_map/all_to_all | solution.py:116
  65.0 22.0 %all-to-all-start.1 = ((f32[20,8,1024]{2,0,1:T(8,128)}), f32[20,8,1024]{2,0,1:T(8,128)S(1)}, u32[]{:S(2)}, u32[]{:S(2)}) async-start(f32[20,8,1024]{2,0,1:T(8,128)} %bitcast.8), calls=%async_computation.1 | async-start | bytes 1572864 | tf_op jit(solution)/shard_map/all_to_all | solution.py:124
  72.3 3.7 %copy-start.6 = (f32[3,8,2,128]{3,1,2,0:T(8,128)S(1)}, f32[3,8,2,128]{3,1,2,0:T(8,128)}, u32[]{:S(2)}) copy-start(f32[3,8,2,128]{3,1,2,0:T(8,128)} %copy-done.5) | copy-start | bytes 73732
  72.3 3.7 %copy-start.7 = (f32[256,256]{1,0:T(8,128)S(1)}, f32[256,256]{1,0:T(8,128)}, u32[]{:S(2)}) copy-start(f32[256,256]{1,0:T(8,128)} %fusion.43) | copy-start | bytes 786436
  72.4 3.7 %copy-start.8 = (f32[20,256]{1,0:T(8,128)S(1)}, f32[20,256]{1,0:T(8,128)}, u32[]{:S(2)}) copy-start(f32[20,256]{1,0:T(8,128)} %param.11) | copy-start | bytes 61444
  72.4 3.7 %copy-start.11 = (pred[256,256]{1,0:T(8,128)(4,1)S(1)}, pred[256,256]{1,0:T(8,128)(4,1)}, u32[]{:S(2)}) copy-start(pred[256,256]{1,0:T(8,128)(4,1)} %fusion.37) | copy-start | bytes 196612
  76.1 12.0 %copy-start.4 = (f32[256,128]{1,0:T(8,128)S(1)}, f32[256,128]{1,0:T(8,128)}, u32[]{:S(2)}) copy-start(f32[256,128]{1,0:T(8,128)} %convert_element_type.21) | copy-start | bytes 393220
  82.3 7.7 %copy-start.15 = (f32[20]{0:T(128)S(1)}, f32[20]{0:T(128)}, u32[]{:S(2)}) copy-start(f32[20]{0:T(128)} %copy-done.14) | copy-start | bytes 244
  82.3 7.7 %copy-start.16 = (f32[20]{0:T(128)S(1)}, f32[20]{0:T(128)}, u32[]{:S(2)}) copy-start(f32[20]{0:T(128)} %slice_reduce_fusion.1) | copy-start | bytes 244
  82.3 7.7 %copy-start.18 = (f32[20]{0:T(128)S(1)}, f32[20]{0:T(128)}, u32[]{:S(2)}) copy-start(f32[20]{0:T(128)} %copy-done.17) | copy-start | bytes 244
  82.3 7.8 %copy-start.19 = (pred[256]{0:T(512)(128)(4,1)S(1)}, pred[256]{0:T(512)(128)(4,1)}, u32[]{:S(2)}) copy-start(pred[256]{0:T(512)(128)(4,1)} %get-tuple-element.159) | copy-start | bytes 772
  91.1 4.6 %copy-start.20 = (f32[20]{0:T(128)S(1)}, f32[20]{0:T(128)}, u32[]{:S(2)}) copy-start(f32[20]{0:T(128)} %get-tuple-element.148) | copy-start | bytes 244
  91.1 4.6 %copy-start.21 = (f32[20]{0:T(128)S(1)}, f32[20]{0:T(128)}, u32[]{:S(2)}) copy-start(f32[20]{0:T(128)} %get-tuple-element.156) | copy-start | bytes 244
  91.1 7.5 %copy-start = (f32[256,20,64]{0,2,1:T(8,128)S(1)}, f32[256,20,64]{0,2,1:T(8,128)}, u32[]{:S(2)}) copy-start(f32[256,20,64]{0,2,1:T(8,128)} %fusion.21) | copy-start | bytes 3932164
  91.1 7.5 %copy-start.3 = (bf16[256,128]{1,0:T(8,128)(2,1)S(1)}, bf16[256,128]{1,0:T(8,128)(2,1)}, u32[]{:S(2)}) copy-start(bf16[256,128]{1,0:T(8,128)(2,1)} %param.13) | copy-start | bytes 196612
  91.1 7.5 %copy-start.9 = (f32[20,256]{1,0:T(8,128)S(1)}, f32[20,256]{1,0:T(8,128)}, u32[]{:S(2)}) copy-start(f32[20,256]{1,0:T(8,128)} %param.11) | copy-start | bytes 61444
  95.6 1.4 %collective-permute-start = (f32[256,128]{1,0:T(8,128)S(1)}, f32[256,128]{1,0:T(8,128)S(1)}, u32[]{:S(2)}, u32[]{:S(2)}) collective-permute-start(f32[256,128]{1,0:T(8,128)S(1)} %fusion.8), channel_id=1, source_target_pairs={{0,1},{1,0},{2,3},{3,2},{4,5},{5,4},{6,7},{7,6},{8,9},{9,8},{10,11... | collective-permute-start | bytes 393224 | tf_op jit(solution)/shard_map/ppermute | solution.py:144
  97.1 23.3 %collective-permute-start.1 = (f32[256,128]{1,0:T(8,128)S(1)}, f32[256,128]{1,0:T(8,128)S(1)}, u32[]{:S(2)}, u32[]{:S(2)}) collective-permute-start(f32[256,128]{1,0:T(8,128)S(1)} %add.61), channel_id=1, source_target_pairs={{0,2},{1,3},{2,0},{3,1},{4,6},{5,7},{6,4},{7,5},{8,10},{9,11},{10,... | collective-permute-start | bytes 393224 | tf_op jit(solution)/shard_map/ppermute | solution.py:144
